TPU v7x, 32 devices: a whole 2x2x4 slice. The times are simulated.
32 devices in a mesh: dp: 4 (over z), expert: 4 (over x, core), etp: 2 (over y).
Axes of the slice: x: 2, y: 2, z: 4, core: 2. Of those that a mesh axis runs over, the one named last changes fastest.
Arguments:
- tokens: bfloat16 [1024, 4096], P(('dp', 'expert')), parts along dimension 0, may hold values from -6 to 6
- expert_ids: int32 [1024, 2], P(('dp', 'expert')), parts along dimension 0, may hold values from 0 to 3, all different within a row; in each aligned block of 64 rows (0 to 63, 64 to 127, ...) at most 64 rows name the same one
- route_weights: bfloat16 [1024, 2], P(('dp', 'expert')), parts along dimension 0, may hold values from 0.049804688 to 1
- w_gate: bfloat16 [4, 4096, 1536], P('expert', None, 'etp'), may hold values from -0.09375 to 0.09375
- w_up: bfloat16 [4, 4096, 1536], P('expert', None, 'etp'), may hold values from -0.09375 to 0.09375
- w_down: bfloat16 [4, 1536, 4096], P('expert', 'etp'), may hold values from -0.15625 to 0.15625
Outputs:
- moe_out: bfloat16 [1024, 4096], P(('dp', 'expert'), 'etp'), parts along dimension 0
There are 4 independent parts, one for each index of `dp`. A program takes and returns all parts, laid end to end along the dimension named above; an argument that names none is the same for every part. Nothing has to cross between parts.
Inputs may be any that keep to these rules, and one draw needn't show every extreme that they name: `expert_ids`: within the 64 rows of one index of expert (aligned blocks), a row names 2 different experts and no expert is named by more than 64 rows; some expert is named by exactly 64 rows of some block.
All inputs are finite; a program needn't handle non-finite values.
Results may differ from a plain program's by a relative error of at most 0.01.
Values may be sent and summed in bfloat16 or wider, within the bound.
A program may use at most 64 MiB of HBM per device.

v0:
```python
import jax
import jax.numpy as jnp
from jax import lax
from jax.sharding import PartitionSpec as P


def per_device(tokens, expert_ids, route_weights, w_gate, w_up, w_down):
    tok_rows, width = tokens.shape
    route_count = expert_ids.shape[1]
    local_experts = w_gate.shape[0]
    sources = lax.axis_size("expert")
    experts = local_experts * sources
    capacity = 2 * tok_rows * route_count // experts
    quarter = width // lax.axis_size("etp")
    flat_ids = expert_ids.reshape(-1)
    onehot = (flat_ids[:, None] == jnp.arange(experts, dtype=jnp.int32)[None, :]).astype(jnp.int32)
    before = jnp.cumsum(onehot, axis=0) - onehot
    slots = jnp.sum(before * onehot, axis=1)
    position = (flat_ids * capacity + slots).reshape(tok_rows, route_count)
    targets = jnp.arange(experts * capacity, dtype=jnp.int32)
    hits = position[:, :, None] == targets[None, None, :]
    dispatch_map = jnp.transpose(jnp.any(hits, axis=1)).astype(jnp.bfloat16)
    combine_map = jnp.sum(
        jnp.where(hits, route_weights[:, :, None], jnp.zeros((), jnp.bfloat16)), axis=1
    )
    outgoing = jnp.dot(dispatch_map, tokens, preferred_element_type=jnp.float32).astype(
        jnp.bfloat16
    )
    arrived = lax.all_to_all(
        outgoing.reshape(experts, capacity, width),
        "expert",
        split_axis=0,
        concat_axis=0,
        tiled=True,
    )
    arrived = arrived.reshape(sources, local_experts, capacity, width)
    gate = jnp.einsum("secd,edh->sech", arrived, w_gate, preferred_element_type=jnp.float32)
    up = jnp.einsum("secd,edh->sech", arrived, w_up, preferred_element_type=jnp.float32)
    hidden = (jax.nn.silu(gate) * up).astype(jnp.bfloat16)
    partial_out = jnp.einsum("sech,ehd->secd", hidden, w_down, preferred_element_type=jnp.float32)
    partial_out = partial_out.reshape(sources * local_experts, capacity, width)
    summed = lax.psum_scatter(
        partial_out.astype(jnp.bfloat16), "etp", scatter_dimension=2, tiled=True
    )
    returned = lax.all_to_all(summed, "expert", split_axis=0, concat_axis=0, tiled=True)
    mixed = jnp.dot(
        combine_map,
        returned.reshape(experts * capacity, quarter),
        preferred_element_type=jnp.float32,
    )
    return mixed.astype(jnp.bfloat16)


def solution(mesh):
    return jax.shard_map(
        per_device,
        mesh=mesh,
        in_specs=(
            P(("dp", "expert"), None),
            P(("dp", "expert"), None),
            P(("dp", "expert"), None),
            P("expert", None, "etp"),
            P("expert", None, "etp"),
            P("expert", "etp", None),
        ),
        out_specs=P(("dp", "expert"), "etp"),
        check_vma=False,
    )
```

profile of v0, /device:TPU:0, one launch (start us, length us, event | category | flops | bytes accessed | tf_op | source)
XLA Modules:
  0.0 110.3 jit_solution(12322868428950840405)
XLA Ops:
  6.5 0.0 copy-start
  6.5 0.0 reduce-scatter.2.cloned.1.call-start
  6.5 0.8 copy.19
  7.4 0.1 eq.28
  7.5 0.1 fusion.30
  7.6 0.2 reduce_window_sum.11
  7.8 0.2 select_reduce_fusion
  7.9 0.1 reduce_sum.24
  8.1 0.1 copy.20
  8.2 0.0 copy-start.2
  8.2 0.8 multiply_add_fusion
  9.0 0.1 fusion.27
  9.1 0.0 copy-done
  9.1 0.7 convolution_convert_fusion
  9.9 29.8 %all_to_all.10 = bf16[4,64,4096]{2,1,0:T(8,128)(2,1)S(1)} all-to-all(bf16[4,64,4096]{2,1,0:T(8,128)(2,1)S(1)} %bitcast.58), channel_id=1, replica_groups=mesh['dp'=4,'expert'=4,'etp'=2] {'expert'}, dimensions={0} | all-to-all | bytes 4194304 | tf_op jit(solution)/shard_map/all_to_all | solution.py:29
  39.7 0.0 copy-done.2
  39.7 1.8 %fusion.9 = f32[4,1,64,768]{3,2,0,1:T(8,128)S(1)} fusion(bf16[4,64,4096]{2,1,0:T(8,128)(2,1)S(1)} %all_to_all.10, bf16[1,4096,768]{2,1,0:T(8,128)(2,1)S(1)} %copy-done.2), kind=kOutput, calls=%fused_computation.9 | convolution fusion | flops 1610612736 | bytes 9175040 | tf_op jit(solution)/shard_map/secd,edh->sech/dot_general | solution.py:37
  41.6 10.6 %fusion.6 = bf16[4,64,4096]{2,1,0:T(8,128)(2,1)} fusion(bf16[1,768,4096]{2,1,0:T(8,128)(2,1)} %param.11, bf16[4,64,4096]{2,1,0:T(8,128)(2,1)S(1)} %all_to_all.10, bf16[1,4096,768]{2,1,0:T(8,128)(2,1)} %param.10, f32[4,1,64,768]{3,2,0,1:T(8,128)S(1)} %fusion.9), kind=kOutput, calls=%fused_computation.7 | convolution fusion | flops 3223453696 | bytes 17563648 | tf_op jit(solution)/shard_map/sech,ehd->secd/dot_general | solution.py:40
  52.1 0.0 copy-start.1
  52.1 0.0 reduce-scatter.2.cloned.1.call-update
  52.1 32.4 %reduce-scatter.2.cloned.1.call-done = bf16[4,64,2048]{2,1,0:T(8,128)(2,1)} async-done(((bf16[4,64,4096]{2,1,0:T(8,128)(2,1)}), bf16[4,64,2048]{2,1,0:T(8,128)(2,1)}) %reduce-scatter.2.cloned.1.call-update) | async-done | bytes 1048592 | tf_op jit(solution)/shard_map/reduce_scatter | solution.py:42
  84.5 3.5 %all-to-all-start.1 = ((bf16[4,64,2048]{2,1,0:T(8,128)(2,1)}), bf16[4,64,2048]{2,1,0:T(8,128)(2,1)S(1)}, u32[]{:S(2)}, u32[]{:S(2)}) async-start(bf16[4,64,2048]{2,1,0:T(8,128)(2,1)} %reduce-scatter.2.cloned.1.call-done), calls=%async_computation.2 | async-start | bytes 2097152 | tf_op jit(solution)/shard_map/all_to_all | solution.py:45
  88.1 0.0 copy-done.1
  88.1 0.1 fusion.29
  88.2 14.3 %all-to-all-done.1 = bf16[4,64,2048]{2,1,0:T(8,128)(2,1)S(1)} async-done(((bf16[4,64,2048]{2,1,0:T(8,128)(2,1)}), bf16[4,64,2048]{2,1,0:T(8,128)(2,1)S(1)}, u32[]{:S(2)}, u32[]{:S(2)}) %all-to-all-start.1) | async-done | bytes 1048608 | tf_op jit(solution)/shard_map/all_to_all | solution.py:45
  102.5 1.0 convolution_convert_fusion.1
Async XLA Ops:
  6.5 2.6 %copy-start = (bf16[64,4096]{1,0:T(8,128)(2,1)S(1)}, bf16[64,4096]{1,0:T(8,128)(2,1)}, u32[]{:S(2)}) copy-start(bf16[64,4096]{1,0:T(8,128)(2,1)} %param.6) | copy-start | bytes 1572868
  6.5 78.0 %reduce-scatter.2.cloned.1.call-start = ((), (), s32[]{:S(2)}) async-start(), calls=%async_computation.3 | async-start | bytes 3145728 | tf_op jit(solution)/shard_map/reduce_scatter | solution.py:42
  8.2 31.5 %copy-start.2 = (bf16[1,4096,768]{2,1,0:T(8,128)(2,1)S(1)}, bf16[1,4096,768]{2,1,0:T(8,128)(2,1)}, u32[]{:S(2)}) copy-start(bf16[1,4096,768]{2,1,0:T(8,128)(2,1)} %param.9) | copy-start | bytes 18874372
  52.1 35.9 %copy-start.1 = (bf16[64,2]{0,1:T(2,128)(2,1)S(1)}, bf16[64,2]{0,1:T(2,128)(2,1)}, u32[]{:S(2)}) copy-start(bf16[64,2]{0,1:T(2,128)(2,1)} %param.8) | copy-start | bytes 772
  84.5 17.9 %all-to-all-start.1 = ((bf16[4,64,2048]{2,1,0:T(8,128)(2,1)}), bf16[4,64,2048]{2,1,0:T(8,128)(2,1)S(1)}, u32[]{:S(2)}, u32[]{:S(2)}) async-start(bf16[4,64,2048]{2,1,0:T(8,128)(2,1)} %reduce-scatter.2.cloned.1.call-done), calls=%async_computation.2 | async-start | bytes 2097152 | tf_op jit(solution)/shard_map/all_to_all | solution.py:45
Sparse Core Ops, SparseCore 0:
  52.3 32.2 reduce-scatter.1
where the time goes:
time: 111 us; the launch traced here: 110 us
  waiting for transfers between devices  46.7 us (42%)
  blocking collectives  29.8 us (27%)
  matrix products  14.1 us (13%)
  between operations  13.5 us (12%)
  starting transfers between devices  3.52 us (3%)
  other arithmetic  1.47 us (1%)
  local copies, waits for them, and re-layouts  1.18 us (1%)
    reduce_scatter x1, waiting for transfers between devices, per_device(): lax.psum_scatter(partial_out.astype(jnp.bfloat16), 'etp', scatter_dimensi...  32.4 us
    all_to_all x1, blocking collectives, per_device(): lax.all_to_all(outgoing.reshape(experts, capacity, width), 'expert', spli...  29.8 us
    all_to_all x1, waiting for transfers between devices, per_device(): lax.all_to_all(summed, 'expert', split_axis=0, concat_axis=0, tiled=True)  14.3 us
    dot_general x1, matrix products, per_device(): jnp.einsum('sech,ehd->secd', hidden, w_down, preferred_element_type=jnp.f...  10.6 us
    all_to_all x1, starting transfers between devices, per_device(): lax.all_to_all(summed, 'expert', split_axis=0, concat_axis=0, tiled=True)  3.51 us
  transfers between devices with their start and end apart: 2, of which 2 were waited for; matrix products, arithmetic and copies ran while one was open for 0% of the time, Pallas kernels for 0%

commit v1 on v0

v1 whole, which is shorter than its diff:
```python
import functools

import jax
import jax.numpy as jnp
from jax import lax
from jax.experimental import pallas as pl
from jax.experimental.pallas import tpu as pltpu
from jax.sharding import PartitionSpec as P

CORES = 2
STEPS = 4
LAG = 3
EARLY = 3


def kernel(
    chips, groups, ids, rw, tok_h, wg_h, wu_h, wd_h, out,
    tok, wg, wu, wd, gacc, uacc, hid, cw, obuf, prec, sbuf, skeep, yrec, xbuf, xrec,
    tok_l, wg_l, wu_l, wd_l, cw_s, cw_r, xs_s, xs_r, pd_s, pd_r, yf_s, yf_r,
    q_s, q_r, ys_s, ys_r, xo_s, xo_r,
):
    experts = chips * CORES
    me = lax.axis_index("expert")
    y = lax.axis_index("etp")
    x, c = me // CORES, lax.rem(me, CORES)
    mate = x * CORES + (1 - c)
    rows, chunk = tok.shape[3], tok.shape[4]
    chunks = STEPS * groups
    f32, bf16 = jnp.float32, jnp.bfloat16

    def remote(src, dst, ss, rs, expert, etp):
        return pltpu.make_async_remote_copy(
            src_ref=src, dst_ref=dst, send_sem=ss, recv_sem=rs,
            device_id={"expert": expert, "etp": etp},
            device_id_type=pl.DeviceIdType.MESH,
        )

    def source(d):
        return lax.rem(x - d + chips, chips)

    def part(dy):
        return lax.rem(y + dy + groups, groups)

    def tok_x(d, j):
        ref = tok.at[x, c, y * STEPS + j]
        return remote(ref, ref, xs_s.at[d, j], xs_r.at[d, j], lax.rem(x + d, chips) * CORES + c, y)

    def tok_x_in(d, j):
        ref = tok.at[source(d), c, y * STEPS + j]
        return remote(ref, ref, xs_s.at[d, j], xs_r.at[d, j], me, y)

    def tok_mate(d, k):
        ref = tok.at[source(d), c, k]
        return remote(ref, ref, pd_s.at[d, k], pd_r.at[d, k], mate, y)

    def tok_mate_in(d, k):
        ref = tok.at[source(d), 1 - c, k]
        return remote(ref, ref, pd_s.at[d, k], pd_r.at[d, k], mate, y)

    def tok_y(d, dy, j):
        ref = tok.at[source(d), c, y * STEPS + j]
        return remote(ref, ref, yf_s.at[d, dy, j], yf_r.at[d, dy, j], me, part(dy))

    def tok_y_in(d, dy, j):
        ref = tok.at[source(d), c, part(-dy) * STEPS + j]
        return remote(ref, ref, yf_s.at[d, dy, j], yf_r.at[d, dy, j], me, part(dy))

    def cw_out(i):
        ref = cw.at[me]
        to = lax.rem(me + i, experts)
        return remote(ref, ref, cw_s.at[i], cw_r.at[i], to, y)

    def cw_in(i):
        ref = cw.at[lax.rem(me - i + experts, experts)]
        return remote(ref, ref, cw_s.at[i], cw_r.at[i], me, y)

    def sum_mate(d, n):
        return remote(obuf.at[d, n, 1 - c], prec.at[d, n], q_s.at[d, n], q_r.at[d, n], mate, y)

    def sum_y(d, dy, j):
        return remote(
            sbuf.at[d, part(dy) * STEPS + j], yrec.at[d, dy, j],
            ys_s.at[d, dy, j], ys_r.at[d, dy, j], me, part(dy),
        )

    def sum_x(d, j):
        return remote(
            xbuf.at[d, j], xrec.at[d, j], xo_s.at[d, j], xo_r.at[d, j], source(d) * CORES + c, y
        )

    def tok_load(k):
        return pltpu.make_async_copy(
            tok_h.at[:, pl.ds(pl.multiple_of(k * chunk, 128), chunk)], tok.at[x, c, k], tok_l.at[k]
        )

    def up_load(k):
        rows_k = pl.ds(k * chunk, chunk)
        return (
            pltpu.make_async_copy(wg_h.at[0, rows_k, :], wg.at[k], wg_l.at[k]),
            pltpu.make_async_copy(wu_h.at[0, rows_k, :], wu.at[k], wu_l.at[k]),
        )

    def down_load(n):
        return pltpu.make_async_copy(
            wd_h.at[0, :, pl.ds(pl.multiple_of(n * chunk, 128), chunk)], wd.at[n], wd_l.at[n]
        )

    own_first = [(dy, j) for dy in range(groups) for j in range(STEPS)]
    own_last = [(dy, j) for dy in list(range(1, groups)) + [0] for j in range(STEPS)]

    barrier = pltpu.get_barrier_semaphore()
    for i in range(1, experts):
        pl.semaphore_signal(
            barrier, inc=1, device_id={"expert": lax.rem(me + i, experts), "etp": y},
            device_id_type=pl.DeviceIdType.MESH,
        )
    for dy in range(1, groups):
        pl.semaphore_signal(
            barrier, inc=1, device_id={"expert": me, "etp": part(dy)},
            device_id_type=pl.DeviceIdType.MESH,
        )
    for dy, j in own_first:
        tok_load(part(dy) * STEPS + j).start()
    for k in range(chunks):
        for copy in up_load(k):
            copy.start()
    for dy, j in own_last:
        down_load(part(dy) * STEPS + j).start()

    lane = lax.broadcasted_iota(jnp.int32, (rows, cw.shape[2]), 1)
    spread = jnp.zeros((rows, cw.shape[2]), f32)
    for k in range(ids.shape[1]):
        spread = spread + jnp.where(lane == ids[:, k : k + 1], rw[:, k : k + 1].astype(f32), 0.0)
    cw[me] = spread

    pl.semaphore_wait(barrier, experts - 1 + groups - 1)
    for dy, j in own_first:
        k = part(dy) * STEPS + j
        tok_load(k).wait()
        if dy == 0:
            for d in range(1, chips):
                tok_x(d, j).start()
    for k in range(chunks):
        tok_mate(0, k).start()

    def relay(d, j):
        tok_x_in(d, j).wait_recv()
        for dy in range(1, groups):
            tok_y(d, dy, j).start()
        tok_mate(d, y * STEPS + j).start()

    def relay_y(d, dy, j):
        tok_y_in(d, dy, j).wait_recv()
        tok_mate(d, part(-dy) * STEPS + j).start()

    def up_step(d, k, first):
        lhs = tok[source(d), :, k].reshape(CORES * rows, chunk)
        g = jnp.dot(lhs, wg[k], preferred_element_type=f32)
        u = jnp.dot(lhs, wu[k], preferred_element_type=f32)
        if first:
            gacc[...] = g
            uacc[...] = u
        else:
            gacc[...] += g
            uacc[...] += u

    def hidden(d):
        for s in range(CORES):
            col = lax.broadcasted_iota(jnp.int32, (rows, cw.shape[2]), 1) == me
            w = jnp.sum(jnp.where(col, cw[source(d) * CORES + s], 0.0), axis=1, keepdims=True)
            g = gacc[s * rows : (s + 1) * rows, :]
            u = uacc[s * rows : (s + 1) * rows, :]
            hid[s * rows : (s + 1) * rows, :] = (g / (1.0 + jnp.exp(-g)) * u * w).astype(bf16)

    def down(d, load, hooks):
        def finish(dy, j):
            n = part(dy) * STEPS + j
            sum_mate(d, n).wait_recv()
            s = obuf[d, n, c].astype(f32) + prec[d, n].astype(f32)
            if dy:
                sbuf[d, n] = s.astype(bf16)
                sum_y(d, dy, j).start()
            else:
                skeep[d, j] = s

        for i, (dy, j) in enumerate(own_last):
            n = part(dy) * STEPS + j
            if load:
                down_load(n).wait()
            o = jnp.dot(hid[...], wd[n], preferred_element_type=f32).astype(bf16)
            obuf[d, n] = o.reshape(CORES, rows, chunk)
            sum_mate(d, n).start()
            if i >= LAG:
                finish(*own_last[i - LAG])
            if i in hooks:
                hooks[i]()
        for i in range(len(own_last) - LAG, len(own_last)):
            finish(*own_last[i])

    for k in range(chunks):
        for copy in up_load(k):
            copy.wait()
        tok_mate_in(0, k).wait_recv()
        up_step(0, k, k == 0)
        if k == 1:
            for i in range(1, experts):
                cw_out(i).start()
    for i in range(1, experts):
        cw_in(i).wait_recv()
    hidden(0)
    early = EARLY if chips > 1 else 0
    hooks = {}
    for e in range(early):
        hooks[chunks * (e + 1) // early - 1] = functools.partial(relay, 1, e)
    down(0, True, hooks)

    def other(d, relayed):
        for j in range(STEPS):
            if j >= relayed:
                relay(d, j)
            if j >= 1:
                for dy in range(1, groups):
                    relay_y(d, dy, j - 1)
            k = y * STEPS + j
            tok_mate_in(d, k).wait_recv()
            up_step(d, k, j == 0)
            if j >= 1:
                for dy in range(1, groups):
                    k = part(-dy) * STEPS + j - 1
                    tok_mate_in(d, k).wait_recv()
                    up_step(d, k, False)
        for dy in range(1, groups):
            relay_y(d, dy, STEPS - 1)
        for dy in range(1, groups):
            k = part(-dy) * STEPS + STEPS - 1
            tok_mate_in(d, k).wait_recv()
            up_step(d, k, False)
        hidden(d)
        down(d, False, {})
        for j in range(STEPS):
            s = skeep[d, j]
            for dy in range(1, groups):
                sum_y(d, dy, j).wait_recv()
                s = s + yrec[d, dy, j].astype(f32)
            xbuf[d, j] = s.astype(bf16)
            sum_x(d, j).start()

    if chips > 1:
        other(1, early)
    if chips > 2:
        lax.fori_loop(2, chips, lambda d, carry: (other(d, 0), carry)[1], 0)

    for j in range(STEPS):
        s = skeep[0, j]
        for dy in range(1, groups):
            sum_y(0, dy, j).wait_recv()
            s = s + yrec[0, dy, j].astype(f32)
        skeep[0, j] = s
    for j in range(STEPS):
        s = skeep[0, j]
        for d in range(1, chips):
            sum_x(d, j).wait_recv()
            s = s + xrec[d, j].astype(f32)
        out[:, j * chunk : (j + 1) * chunk] = s.astype(bf16)

    for i in range(1, experts):
        cw_out(i).wait_send()
    for d in range(chips):
        for n in range(chunks):
            tok_mate(d, n).wait_send()
            sum_mate(d, n).wait_send()
        for j in range(STEPS):
            for dy in range(1, groups):
                sum_y(d, dy, j).wait_send()
            if d:
                tok_x(d, j).wait_send()
                sum_x(d, j).wait_send()
                for dy in range(1, groups):
                    tok_y(d, dy, j).wait_send()


def solution(mesh):
    chips = mesh.shape["expert"] // CORES
    groups = mesh.shape["etp"]
    experts = chips * CORES
    chunks = STEPS * groups

    def per_device(tokens, expert_ids, route_weights, w_gate, w_up, w_down):
        rows, width = tokens.shape
        units = w_gate.shape[2]
        chunk = width // chunks
        lanes = -(-experts // 128) * 128
        bf16, f32 = jnp.bfloat16, jnp.float32
        vmem, dma = pltpu.VMEM, pltpu.SemaphoreType.DMA
        any_spec = pl.BlockSpec(memory_space=pl.ANY)
        vmem_spec = pl.BlockSpec(memory_space=pltpu.VMEM)
        return pl.pallas_call(
            functools.partial(kernel, chips, groups),
            out_shape=jax.ShapeDtypeStruct((rows, width // groups), bf16),
            in_specs=[vmem_spec, vmem_spec] + [any_spec] * 4,
            out_specs=vmem_spec,
            scratch_shapes=[
                vmem((chips, CORES, chunks, rows, chunk), bf16),
                vmem((chunks, chunk, units), bf16),
                vmem((chunks, chunk, units), bf16),
                vmem((chunks, units, chunk), bf16),
                vmem((CORES * rows, units), f32),
                vmem((CORES * rows, units), f32),
                vmem((CORES * rows, units), bf16),
                vmem((experts, rows, lanes), f32),
                vmem((chips, chunks, CORES, rows, chunk), bf16),
                vmem((chips, chunks, rows, chunk), bf16),
                vmem((chips, chunks, rows, chunk), bf16),
                vmem((chips, STEPS, rows, chunk), f32),
                vmem((chips, groups, STEPS, rows, chunk), bf16),
                vmem((chips, STEPS, rows, chunk), bf16),
                vmem((chips, STEPS, rows, chunk), bf16),
                dma((chunks,)), dma((chunks,)), dma((chunks,)), dma((chunks,)),
                dma((experts,)), dma((experts,)),
                dma((chips, STEPS)), dma((chips, STEPS)),
                dma((chips, chunks)), dma((chips, chunks)),
                dma((chips, groups, STEPS)), dma((chips, groups, STEPS)),
                dma((chips, chunks)), dma((chips, chunks)),
                dma((chips, groups, STEPS)), dma((chips, groups, STEPS)),
                dma((chips, STEPS)), dma((chips, STEPS)),
            ],
            compiler_params=pltpu.CompilerParams(
                collective_id=0, has_side_effects=True, vmem_limit_bytes=60 * 1024 * 1024
            ),
        )(expert_ids, route_weights, tokens, w_gate, w_up, w_down)

    return jax.shard_map(
        per_device,
        mesh=mesh,
        in_specs=(
            P(("dp", "expert"), None),
            P(("dp", "expert"), None),
            P(("dp", "expert"), None),
            P("expert", None, "etp"),
            P("expert", None, "etp"),
            P("expert", "etp", None),
        ),
        out_specs=P(("dp", "expert"), "etp"),
        check_vma=False,
    )
```

time: 111 us -> 47.3 us (0.43)
  waiting for transfers between devices: 46.7 us -> 0 us
  Pallas kernels: 0 us -> 42.6 us
  blocking collectives: 29.8 us -> 0 us
  matrix products: 14.1 us -> 0 us
  between operations: 13.5 us -> 0.01 us
  starting transfers between devices: 3.52 us -> 0 us
  local copies, waits for them, and re-layouts: 1.18 us -> 4.4 us
  other arithmetic: 1.47 us -> 0 us
    pallas_call x0 -> x1, Pallas kernels: none -> 42.6 us  [per_device(): pl.pallas_call(functools.partial(kernel, chips, groups), out_shape=jax.Sh...]
    reduce_scatter x1 -> x0, waiting for transfers between devices: 32.4 us -> none  [per_device(): lax.psum_scatter(partial_out.astype(jnp.bfloat16), 'etp', scatter_dimensi...]
    all_to_all x1 -> x0, blocking collectives: 29.8 us -> none  [per_device(): lax.all_to_all(outgoing.reshape(experts, capacity, width), 'expert', spli...]
    all_to_all x1 -> x0, waiting for transfers between devices: 14.3 us -> none  [per_device(): lax.all_to_all(summed, 'expert', split_axis=0, concat_axis=0, tiled=True)]
    dot_general x4 -> x0, matrix products: 14.1 us -> none  [the longest x1 10.6 us: per_device(): jnp.einsum('sech,ehd->secd', hidden, w_down, preferred_element_type=jnp.f...]
    unnamed x7 -> x3, local copies, waits for them, and re-layouts: 0.84 us -> 4.4 us
    all_to_all x1 -> x0, starting transfers between devices: 3.51 us -> none  [per_device(): lax.all_to_all(summed, 'expert', split_axis=0, concat_axis=0, tiled=True)]
  transfers between devices with their start and end apart: 2 -> 0, of which waited for: 2 -> 0; matrix products, arithmetic and copies ran while one was open for 0% -> 0% of each run, Pallas kernels for 0% -> 0%
where the time goes in v1:
time: 47.3 us; the launch traced here: 47 us
  Pallas kernels  42.6 us (90%)
  local copies, waits for them, and re-layouts  4.4 us (9%)
    pallas_call x1, Pallas kernels, per_device(): pl.pallas_call(functools.partial(kernel, chips, groups), out_shape=jax.Sh...  42.6 us
    unnamed x3, local copies, waits for them, and re-layouts  4.4 us

profile of v1, /device:TPU:0, one launch (start us, length us, event | category | flops | bytes accessed | tf_op | source)
XLA Modules:
  0.0 47.0 jit_solution(3623567724939700637)
XLA Ops:
  0.0 1.3 %copy.8.rw = bf16[64,2]{1,0:T(8,128)(2,1)} copy(bf16[64,2]{0,1:T(2,128)(2,1)} %param.8) | data formatting | bytes 512 | tf_op args[2]
  1.4 1.4 %copy.7.ids = s32[64,2]{1,0:T(8,128)} copy(s32[64,2]{0,1:T(2,128)} %param.7) | data formatting | bytes 1024 | tf_op args[1]
  2.7 42.6 %shard_map.64 = bf16[64,2048]{1,0:T(8,128)(2,1)} custom-call(s32[64,2]{1,0:T(8,128)} %copy.7.ids, bf16[64,2]{1,0:T(8,128)(2,1)} %copy.8.rw, bf16[64,4096]{1,0:T(8,128)(2,1)} %tok_h.1, bf16[1,4096,768]{2,1,0:T(8,128)(2,1)} %wg_h.1, bf16[1,4096,768]{2,1,0:T(8,128)(2,1)} %wu_h.1, bf16[1,768,4096]{2,1,0:T(8,128)(2,1)} %wd_h.1), custom_call_target="tpu_custom_call" | custom-call | tf_op jit(solution)/shard_map/pallas_call | solution.py:297
  45.4 1.7 %copy.10 = bf16[64,2048]{1,0:T(8,128)(2,1)} copy(bf16[64,2048]{1,0:T(8,128)(2,1)} %shard_map.64) | data formatting | bytes 524288

commit v2 on v1

--- a/solution.py
+++ b/solution.py
@@ -8,9 +8,11 @@
 from jax.sharding import PartitionSpec as P
 
 CORES = 2
-STEPS = 4
-LAG = 3
-EARLY = 3
+STEPS = 2
+RELAYED = 1
+LAG = 2
+UP_RELAYS = (2,)
+DOWN_RELAYS = (0,)
 
 
 def kernel(
@@ -58,11 +60,18 @@
         return remote(ref, ref, pd_s.at[d, k], pd_r.at[d, k], mate, y)
 
     def tok_y(d, dy, j):
+        if j >= RELAYED:
+            ref = tok.at[x, c, part(dy) * STEPS + j]
+            to = lax.rem(x + d, chips) * CORES + c
+            return remote(ref, ref, yf_s.at[d, dy, j], yf_r.at[d, dy, j], to, y)
         ref = tok.at[source(d), c, y * STEPS + j]
         return remote(ref, ref, yf_s.at[d, dy, j], yf_r.at[d, dy, j], me, part(dy))
 
+    def far(dy, j):
+        return part(dy if j >= RELAYED else -dy) * STEPS + j
+
     def tok_y_in(d, dy, j):
-        ref = tok.at[source(d), c, part(-dy) * STEPS + j]
+        ref = tok.at[source(d), c, far(dy, j)]
         return remote(ref, ref, yf_s.at[d, dy, j], yf_r.at[d, dy, j], me, part(dy))
 
     def cw_out(i):
@@ -127,31 +136,38 @@
     for dy, j in own_last:
         down_load(part(dy) * STEPS + j).start()
 
-    lane = lax.broadcasted_iota(jnp.int32, (rows, cw.shape[2]), 1)
-    spread = jnp.zeros((rows, cw.shape[2]), f32)
-    for k in range(ids.shape[1]):
-        spread = spread + jnp.where(lane == ids[:, k : k + 1], rw[:, k : k + 1].astype(f32), 0.0)
+    named = lax.broadcasted_iota(jnp.int32, (cw.shape[1], rows), 0)
+    spread = jnp.zeros((cw.shape[1], rows), f32)
+    for k in range(ids.shape[0]):
+        spread = spread + jnp.where(named == ids[k : k + 1, :], rw[k : k + 1, :].astype(f32), 0.0)
     cw[me] = spread
 
     pl.semaphore_wait(barrier, experts - 1 + groups - 1)
+    for i in range(1, experts):
+        cw_out(i).start()
     for dy, j in own_first:
         k = part(dy) * STEPS + j
         tok_load(k).wait()
         if dy == 0:
             for d in range(1, chips):
                 tok_x(d, j).start()
+    for d in range(1, chips):
+        for dy in range(1, groups):
+            for j in range(RELAYED, STEPS):
+                tok_y(d, dy, j).start()
     for k in range(chunks):
         tok_mate(0, k).start()
 
     def relay(d, j):
         tok_x_in(d, j).wait_recv()
-        for dy in range(1, groups):
-            tok_y(d, dy, j).start()
+        if j < RELAYED:
+            for dy in range(1, groups):
+                tok_y(d, dy, j).start()
         tok_mate(d, y * STEPS + j).start()
 
     def relay_y(d, dy, j):
         tok_y_in(d, dy, j).wait_recv()
-        tok_mate(d, part(-dy) * STEPS + j).start()
+        tok_mate(d, far(dy, j)).start()
 
     def up_step(d, k, first):
         lhs = tok[source(d), :, k].reshape(CORES * rows, chunk)
@@ -166,8 +182,11 @@
 
     def hidden(d):
         for s in range(CORES):
-            col = lax.broadcasted_iota(jnp.int32, (rows, cw.shape[2]), 1) == me
-            w = jnp.sum(jnp.where(col, cw[source(d) * CORES + s], 0.0), axis=1, keepdims=True)
+            mine = lax.broadcasted_iota(jnp.int32, (cw.shape[1], rows), 0) == me
+            line = jnp.sum(jnp.where(mine, cw[source(d) * CORES + s], 0.0), axis=0, keepdims=True)
+            down_ = lax.broadcasted_iota(jnp.int32, (rows, rows), 0)
+            along = lax.broadcasted_iota(jnp.int32, (rows, rows), 1)
+            w = jnp.sum(jnp.where(down_ == along, line, 0.0), axis=1, keepdims=True)
             g = gacc[s * rows : (s + 1) * rows, :]
             u = uacc[s * rows : (s + 1) * rows, :]
             hid[s * rows : (s + 1) * rows, :] = (g / (1.0 + jnp.exp(-g)) * u * w).astype(bf16)
@@ -202,16 +221,16 @@
             copy.wait()
         tok_mate_in(0, k).wait_recv()
         up_step(0, k, k == 0)
-        if k == 1:
-            for i in range(1, experts):
-                cw_out(i).start()
+        if chips > 1 and k in UP_RELAYS:
+            relay(1, UP_RELAYS.index(k))
     for i in range(1, experts):
         cw_in(i).wait_recv()
     hidden(0)
-    early = EARLY if chips > 1 else 0
+    early = len(UP_RELAYS) + len(DOWN_RELAYS) if chips > 1 else 0
     hooks = {}
-    for e in range(early):
-        hooks[chunks * (e + 1) // early - 1] = functools.partial(relay, 1, e)
+    if chips > 1:
+        for e, i in enumerate(DOWN_RELAYS):
+            hooks[i] = functools.partial(relay, 1, len(UP_RELAYS) + e)
     down(0, True, hooks)
 
     def other(d, relayed):
@@ -226,13 +245,13 @@
             up_step(d, k, j == 0)
             if j >= 1:
                 for dy in range(1, groups):
-                    k = part(-dy) * STEPS + j - 1
+                    k = far(dy, j - 1)
                     tok_mate_in(d, k).wait_recv()
                     up_step(d, k, False)
         for dy in range(1, groups):
             relay_y(d, dy, STEPS - 1)
         for dy in range(1, groups):
-            k = part(-dy) * STEPS + STEPS - 1
+            k = far(dy, STEPS - 1)
             tok_mate_in(d, k).wait_recv()
             up_step(d, k, False)
         hidden(d)
@@ -289,7 +308,6 @@
         rows, width = tokens.shape
         units = w_gate.shape[2]
         chunk = width // chunks
-        lanes = -(-experts // 128) * 128
         bf16, f32 = jnp.bfloat16, jnp.float32
         vmem, dma = pltpu.VMEM, pltpu.SemaphoreType.DMA
         any_spec = pl.BlockSpec(memory_space=pl.ANY)
@@ -307,7 +325,7 @@
                 vmem((CORES * rows, units), f32),
                 vmem((CORES * rows, units), f32),
                 vmem((CORES * rows, units), bf16),
-                vmem((experts, rows, lanes), f32),
+                vmem((experts, -(-experts // 8) * 8, rows), f32),
                 vmem((chips, chunks, CORES, rows, chunk), bf16),
                 vmem((chips, chunks, rows, chunk), bf16),
                 vmem((chips, chunks, rows, chunk), bf16),
@@ -327,7 +345,7 @@
             compiler_params=pltpu.CompilerParams(
                 collective_id=0, has_side_effects=True, vmem_limit_bytes=60 * 1024 * 1024
             ),
-        )(expert_ids, route_weights, tokens, w_gate, w_up, w_down)
+        )(expert_ids.T, route_weights.T, tokens, w_gate, w_up, w_down)
 
     return jax.shard_map(
         per_device,

time: 47.3 us -> 35.6 us (0.75)
  Pallas kernels: 42.6 us -> 33.8 us
  local copies, waits for them, and re-layouts: 4.4 us -> 1.67 us
    pallas_call x1, Pallas kernels: 42.6 us -> 33.8 us  [per_device(): pl.pallas_call(functools.partial(kernel, chips, groups), out_shape=jax.Sh...]
    unnamed x3 -> x1, local copies, waits for them, and re-layouts: 4.4 us -> 1.67 us
where the time goes in v2:
time: 35.6 us; the launch traced here: 35.5 us
  Pallas kernels  33.8 us (95%)
  local copies, waits for them, and re-layouts  1.67 us (5%)
    pallas_call x1, Pallas kernels, per_device(): pl.pallas_call(functools.partial(kernel, chips, groups), out_shape=jax.Sh...  33.8 us
    unnamed x1, local copies, waits for them, and re-layouts  1.67 us

profile of v2, /device:TPU:0, one launch (start us, length us, event | category | flops | bytes accessed | tf_op | source)
XLA Modules:
  0.0 35.5 jit_solution(2553569332808021811)
XLA Ops:
  0.0 33.8 %shard_map.64 = bf16[64,2048]{1,0:T(8,128)(2,1)} custom-call(s32[2,64]{1,0:T(2,128)} %bitcast.2, bf16[2,64]{1,0:T(2,128)(2,1)} %bitcast.3, bf16[64,4096]{1,0:T(8,128)(2,1)} %tok_h.1, bf16[1,4096,768]{2,1,0:T(8,128)(2,1)} %wg_h.1, bf16[1,4096,768]{2,1,0:T(8,128)(2,1)} %wu_h.1, bf16[1,768,4096]{2,1,0:T(8,128)(2,1)} %wd_h.1), custom_call_target="tpu_custom_call" | custom-call | tf_op jit(solution)/shard_map/pallas_call | solution.py:315
  33.8 1.7 %copy.8 = bf16[64,2048]{1,0:T(8,128)(2,1)} copy(bf16[64,2048]{1,0:T(8,128)(2,1)} %shard_map.64) | data formatting | bytes 524288
